TPU v7x, 32 devices: a 4x4x1 block of a 4x4x8 slice. The times are simulated.
32 devices in a mesh: dp: 1 (over z), tp: 32 (over x, y, core).
Axes of the slice: x: 4, y: 4, z: 1, core: 2. Of those that a mesh axis runs over, the one named last changes fastest.
The devices are a block of a 4x4x8 slice.
Arguments:
- x: bfloat16 [2048, 7168], P('dp')
- dy: bfloat16 [2048, 7168], P('dp')
- gate: bfloat16 [2048, 20480], P('dp', 'tp')
- up: bfloat16 [2048, 20480], P('dp', 'tp')
- w_gate: bfloat16 [7168, 20480], P(None, 'tp')
- w_up: bfloat16 [7168, 20480], P(None, 'tp')
- w_down: bfloat16 [20480, 7168], P('tp')
Outputs:
- output 1: bfloat16 [2048, 7168], P('dp')
- output 2: bfloat16 [7168, 20480], P('dp', 'tp')
- output 3: bfloat16 [7168, 20480], P('dp', 'tp')
- output 4: bfloat16 [20480, 7168], P(('dp', 'tp'))
All inputs are finite; a program needn't handle non-finite values.
Results may differ from a plain program's by a relative error of at most 0.012.
Values are sent between devices in bfloat16 or wider.
A program may use at most 768 MiB of HBM per device.

v0:
```python
import jax
import jax.numpy as jnp
from jax import lax
from jax.sharding import PartitionSpec as P


def act(gate, up):
    return jax.nn.silu(gate) * up


def solution(mesh):
    def step(x, dy, gate, up, w_gate, w_up, w_down):
        hidden, back = jax.vjp(act, gate.astype(jnp.float32), up.astype(jnp.float32))
        d_hidden = jnp.dot(dy, w_down.T, preferred_element_type=jnp.float32)
        d_gate, d_up = (g.astype(jnp.bfloat16) for g in back(d_hidden))
        term = jnp.dot(d_gate, w_gate.T, preferred_element_type=jnp.float32) + jnp.dot(d_up, w_up.T, preferred_element_type=jnp.float32)
        dx = lax.psum(term.astype(jnp.bfloat16), "tp")
        dw_gate = jnp.dot(x.T, d_gate, preferred_element_type=jnp.float32)
        dw_up = jnp.dot(x.T, d_up, preferred_element_type=jnp.float32)
        dw_down = jnp.dot(hidden.astype(jnp.bfloat16).T, dy, preferred_element_type=jnp.float32)
        return dx, *(g.astype(jnp.bfloat16) for g in (dw_gate, dw_up, dw_down))

    tokens, columns, rows = P("dp", None), P(None, "tp"), P("tp", None)
    return jax.shard_map(
        step,
        mesh=mesh,
        in_specs=(tokens, tokens, P("dp", "tp"), P("dp", "tp"), columns, columns, rows),
        out_specs=(tokens, P("dp", "tp"), P("dp", "tp"), P(("dp", "tp"), None)),
        check_vma=False,
    )
```

profile of v0, /device:TPU:97, one launch (start us, length us, event | category | flops | bytes accessed | tf_op | source)
XLA Modules:
  0.0 355.6 jit_solution(1982151255093328392)
XLA Ops:
  7.2 0.1 all-reduce.2.cloned.1.call-start
  7.2 32.2 %fusion.8 = (bf16[2048,640]{1,0:T(8,128)(2,1)}, f32[2048,640]{1,0:T(8,128)}) fusion(bf16[2048,640]{1,0:T(8,128)(2,1)} %param.9, bf16[2048,640]{1,0:T(8,128)(2,1)} %param.10, bf16[2048,7168]{1,0:T(8,128)(2,1)} %param.8, bf16[640,7168]{1,0:T(8,128)(2,1)} %param.13), kind=kOutput, calls=%fused_computation.18 | convolution fusion | flops 18807521280 | bytes 51642368 | tf_op jit(solution)/shard_map/dot_general | solution.py:14
  39.4 0.0 copy-start
  39.4 32.7 %fusion.11 = f32[2048,7168]{1,0:T(8,128)} fusion(bf16[2048,640]{1,0:T(8,128)(2,1)} %get-tuple-element.8, bf16[7168,640]{1,0:T(8,128)(2,1)} %param.11), kind=kOutput, calls=%fused_computation.21 | convolution fusion | flops 18790481920 | bytes 70516736 | tf_op jit(solution)/shard_map/dot_general | solution.py:16
  72.1 0.0 copy-done
  72.1 42.5 %add_convert_fusion = bf16[2048,7168]{1,0:T(8,128)(2,1)} fusion(f32[2048,7168]{1,0:T(8,128)} %fusion.11, bf16[7168,640]{1,0:T(8,128)(2,1)} %param.12, f32[2048,640]{1,0:T(8,128)} %get-tuple-element.9, bf16[2048,640]{1,0:T(8,128)(2,1)S(1)} %copy-done), kind=kOutput, calls=%fused_computation | convolution fusion | flops 18829017088 | bytes 105119744 | tf_op jit(solution)/shard_map/dot_general | solution.py:16
  114.6 0.1 all-reduce.2.cloned.1.call-update
  114.7 27.3 %fusion = bf16[7168,640]{0,1:T(8,128)(2,1)} fusion(bf16[2048,640]{1,0:T(8,128)(2,1)} %get-tuple-element.8, bf16[2048,7168]{1,0:T(8,128)(2,1)} %param.7), kind=kOutput, calls=%fused_computation.4 | convolution fusion | flops 18795069440 | bytes 41156608 | tf_op jit(solution)/shard_map/dot_general | solution.py:18
  142.0 12.7 %copy.11 = bf16[7168,640]{1,0:T(8,128)(2,1)} copy(bf16[7168,640]{0,1:T(8,128)(2,1)} %fusion) | data formatting | bytes 18350080
  154.6 28.7 %fusion.1 = bf16[7168,640]{0,1:T(8,128)(2,1)} fusion(bf16[2048,7168]{1,0:T(8,128)(2,1)} %param.7, f32[2048,640]{1,0:T(8,128)} %get-tuple-element.9, bf16[2048,640]{1,0:T(8,128)(2,1)S(1)} %copy-done), kind=kOutput, calls=%fused_computation.5 | convolution fusion | flops 18804244480 | bytes 46399488 | tf_op jit(solution)/shard_map/dot_general | solution.py:19
  183.3 12.7 %copy.12 = bf16[7168,640]{1,0:T(8,128)(2,1)} copy(bf16[7168,640]{0,1:T(8,128)(2,1)} %fusion.1) | data formatting | bytes 18350080
  196.0 28.9 %convolution_convert_fusion = bf16[640,7168]{1,0:T(8,128)(2,1)} fusion(bf16[2048,7168]{1,0:T(8,128)(2,1)} %param.8, bf16[2048,640]{1,0:T(8,128)(2,1)} %param.10, bf16[2048,640]{1,0:T(8,128)(2,1)S(1)} %copy-done), kind=kOutput, calls=%fused_computation.1 | convolution fusion | flops 18805555200 | bytes 43778048 | tf_op jit(solution)/shard_map/dot_general | solution.py:20
  224.8 103.8 %all-reduce.2.cloned.1.call-done = bf16[2048,7168]{1,0:T(8,128)(2,1)} async-done(((bf16[2048,7168]{1,0:T(8,128)(2,1)}), bf16[2048,7168]{1,0:T(8,128)(2,1)}) %all-reduce.2.cloned.1.call-update) | async-done | bytes 29360144 | tf_op jit(solution)/shard_map/psum | solution.py:17
  328.6 20.1 %copy.14 = bf16[2048,7168]{1,0:T(8,128)(2,1)} copy(bf16[2048,7168]{1,0:T(8,128)(2,1)} %all-reduce.2.cloned.1.call-done) | data formatting | bytes 58720256
Async XLA Ops:
  7.2 321.4 %all-reduce.2.cloned.1.call-start = ((), (), s32[]{:S(2)}) async-start(), calls=%async_computation | async-start | bytes 58720256 | tf_op jit(solution)/shard_map/psum | solution.py:17
  39.4 32.7 %copy-start = (bf16[2048,640]{1,0:T(8,128)(2,1)S(1)}, bf16[2048,640]{1,0:T(8,128)(2,1)}, u32[]{:S(2)}) copy-start(bf16[2048,640]{1,0:T(8,128)(2,1)} %param.9) | copy-start | bytes 7864324
Sparse Core Ops, SparseCore 0:
  114.8 213.7 all-reduce.1
where the time goes:
time: 356 us
  matrix products  192 us (54%)
  waiting for transfers between devices  104 us (29%)
  local copies, waits for them, and re-layouts  45.5 us (13%)
  between operations  14.1 us (4%)
    psum x1, waiting for transfers between devices, step(): dx = lax.psum(term.astype(jnp.bfloat16), 'tp')  104 us
    unnamed x5, local copies, waits for them, and re-layouts  45.5 us
    dot_general x1, matrix products, step(): jnp.dot(d_up, w_up.T, preferred_element_type=jnp.float32)  42.5 us
    dot_general x1, matrix products, step(): jnp.dot(d_gate, w_gate.T, preferred_element_type=jnp.float32)  32.7 us
    dot_general x1, matrix products, step(): d_hidden = jnp.dot(dy, w_down.T, preferred_element_type=jnp.float32)  32.2 us
    dot_general x1, matrix products, step(): jnp.dot(hidden.astype(jnp.bfloat16).T, dy, preferred_element_type=jnp.flo...  28.9 us
    dot_general x1, matrix products, step(): dw_up = jnp.dot(x.T, d_up, preferred_element_type=jnp.float32)  28.7 us
    dot_general x1, matrix products, step(): dw_gate = jnp.dot(x.T, d_gate, preferred_element_type=jnp.float32)  27.3 us
  transfers between devices with their start and end apart: 1, of which 1 were waited for; matrix products, arithmetic and copies ran while one was open for 31% of the time, Pallas kernels for 0%

commit v1 on v0

v1 whole, which is shorter than its diff:
```python
import functools

import jax
import jax.numpy as jnp
from jax import lax
from jax.experimental import pallas as pl
from jax.experimental.pallas import tpu as pltpu
from jax.sharding import PartitionSpec as P

MESH = pl.DeviceIdType.MESH
BF16, F32 = jnp.bfloat16, jnp.float32
R = 256
L = 128
SIDE = 4
GROUPS = 2
NT = (((1,), (1,)), ((), ()))
VMEM_LIMIT = 66_900_000


def reduce_kernel(
    nch, dy, gate, up, wg, wu, wd, grads, *rest
):
    outs = rest[:GROUPS]
    (w, wdv, dyv, gv, uv, dh, dt, obuf, pbuf, cs, s1a, r1a, s1b, r1b, p1, s2a, r2a, s2b, r2b, fin,
     in_sem, w_sem, dt_sem, fin_sem, ps, pr, ss1a, sr1a, ss1b, sr1b, ss2a, sr2a, ss2b, sr2b,
     cp, c1a, c1b, c2a, c2b) = rest[GROUPS:]
    f = wg.shape[1]
    half = wg.shape[0] // 2
    quarter = half // SIDE
    sub = quarter // SIDE
    hs = sub // 2
    per_group = nch // GROUPS

    me = lax.axis_index("tp")
    core = lax.rem(me, 2)
    y = lax.rem(me // 2, SIDE)
    x = me // (2 * SIDE)

    def at(i, j, c):
        return (lax.rem(i + SIDE, SIDE) * SIDE + lax.rem(j + SIDE, SIDE)) * 2 + c

    partner = at(x, y, 1 - core)
    xn = (at(x + 1, y, core), at(x - 1, y, core))
    yn = (at(x, y + 1, core), at(x, y - 1, core))
    ring1, pos1 = (xn, yn), (x, y)
    ring2, pos2 = (yn, xn), (y, x)

    def fetch(k):
        rows = pl.ds(pl.multiple_of(k * R, R), R)
        return [
            pltpu.make_async_copy(dy.at[rows], dyv, in_sem.at[0]),
            pltpu.make_async_copy(gate.at[rows], gv, in_sem.at[1]),
            pltpu.make_async_copy(up.at[rows], uv, in_sem.at[2]),
        ]

    wcopies = [
        pltpu.make_async_copy(wd, wdv, w_sem.at[0]),
        pltpu.make_async_copy(wg, w.at[:, pl.ds(0, f)], w_sem.at[1]),
        pltpu.make_async_copy(wu, w.at[:, pl.ds(f, f)], w_sem.at[2]),
    ]
    first = fetch(0)
    first[0].start()
    wcopies[0].start()
    first[1].start()
    first[2].start()
    wcopies[1].start()
    wcopies[2].start()

    barrier = pltpu.get_barrier_semaphore()
    for peer in (partner, *xn, *yn):
        pl.semaphore_signal(barrier, inc=1, device_id={"tp": peer}, device_id_type=MESH)
    pl.semaphore_wait(barrier, 5)

    def remote(src, dst, ssem, rsem, dev):
        return pltpu.make_async_remote_copy(
            src_ref=src, dst_ref=dst, send_sem=ssem, recv_sem=rsem,
            device_id={"tp": dev}, device_id_type=MESH,
        )

    def pair_copy(k, a):
        s = lax.rem(k, 2)
        return remote(obuf.at[s, a], pbuf.at[s, a], ps.at[s, a], pr.at[s, a], partner)

    def hop(k, c, d, src, dst, ssem, rsem, ring):
        s = lax.rem(k, 2)
        return remote(src.at[s, c, d], dst.at[s, c, d], ssem.at[s, c, d], rsem.at[s, c, d], ring[c][d])

    h1a = lambda k, c, d: hop(k, c, d, s1a, r1a, ss1a, sr1a, ring1)
    h1b = lambda k, c, d: hop(k, c, d, s1b, r1b, ss1b, sr1b, ring1)
    h2a = lambda k, c, d: hop(k, c, d, s2a, r2a, ss2a, sr2a, ring2)
    h2b = lambda k, c, d: hop(k, c, d, s2b, r2b, ss2b, sr2b, ring2)
    CD = [(c, d) for c in range(2) for d in range(2)]

    def before_fill(k, h):
        @pl.when(k >= 2)
        def _():
            for c, d in CD:
                h(k - 2, c, d).wait_send()

    def launch(k, h, credit):
        @pl.when(k >= 2)
        def _():
            for c, d in CD:
                pl.semaphore_wait(credit.at[c, d], 1)
        for c, d in CD:
            h(k, c, d).start()

    def give_credit(k, credit, ring):
        @pl.when(k + 2 < nch)
        def _():
            for c, d in CD:
                pl.semaphore_signal(
                    credit.at[c, d], inc=1, device_id={"tp": ring[c][1 - d]}, device_id_type=MESH
                )

    def ring_at(p, off):
        return lax.rem(p + off, SIDE)

    def piece(s, c, q):
        if c == 0:
            return lambda lo, n: cs[s, q, pl.ds(lo, n), :, pl.ds(0, L)]
        return lambda lo, n: cs[s, pl.ds(lo, n), q, :, pl.ds(L, L)]

    def grads_copy(k):
        s = lax.rem(k, 2)
        return pltpu.make_async_copy(
            dt.at[s], grads.at[:, pl.ds(pl.multiple_of(k * R, R), R)], dt_sem.at[s]
        )

    def stage_a(k):
        s = lax.rem(k, 2)
        for c in fetch(k):
            c.wait()

        @pl.when(k == 0)
        def _():
            wcopies[0].wait()

        depth = dyv.shape[1] // 4
        dh[...] = jnp.zeros_like(dh)

        @pl.loop(0, 4)
        def _(j):
            cols = pl.ds(pl.multiple_of(j * depth, depth), depth)
            dh[...] += lax.dot_general(wdv[:, cols], dyv[:, cols], NT, preferred_element_type=F32)

        @pl.when(k >= 2)
        def _():
            grads_copy(k - 2).wait()

        g = gv[...].astype(F32).T
        u = uv[...].astype(F32).T
        d = dh[...]
        sig = 1.0 / (1.0 + jnp.exp(-g))
        silu = g * sig
        dt[s, pl.ds(2 * f, f)] = (silu * u).astype(BF16)
        dt[s, pl.ds(f, f)] = (d * silu).astype(BF16)
        dt[s, pl.ds(0, f)] = (d * u * (sig + silu * (1.0 - sig))).astype(BF16)
        grads_copy(k).start()

        @pl.when(k + 1 < nch)
        def _():
            for c in fetch(k + 1):
                c.start()

    def rows_of(h, a):
        return pl.ds(pl.multiple_of(h * half + a * quarter, quarter), quarter)

    def stage_b(k):
        s = lax.rem(k, 2)

        @pl.when(k == 0)
        def _():
            wcopies[1].wait()
            wcopies[2].wait()

        @pl.when(k >= 2)
        def _():
            pl.semaphore_wait(cp, 1)

        @pl.loop(0, SIDE)
        def _(a):
            @pl.when(k >= 2)
            def _():
                pair_copy(k - 2, a).wait_send()

            t = jnp.dot(w[rows_of(1 - core, a)], dt[s, pl.ds(0, 2 * f)], preferred_element_type=F32)
            obuf[s, a] = t.astype(BF16).reshape(SIDE, sub, R)
            pair_copy(k, a).start()

    def stage_c(k):
        s = lax.rem(k, 2)

        @pl.loop(0, SIDE)
        def _(a):
            t = jnp.dot(w[rows_of(core, a)], dt[s, pl.ds(0, 2 * f)], preferred_element_type=F32)
            pair_copy(k, a).wait_recv()
            cs[s, a] = t.reshape(SIDE, sub, R) + pbuf[s, a].astype(F32)

        @pl.when(k + 2 < nch)
        def _():
            pl.semaphore_signal(cp, inc=1, device_id={"tp": partner}, device_id_type=MESH)

    def stage_1a(k):
        s = lax.rem(k, 2)
        before_fill(k, h1a)
        for c in range(2):
            take = piece(s, c, ring_at(pos1[c], 2))
            for d in range(2):
                s1a[s, c, d] = take(2 * d, 2).astype(BF16)
        launch(k, h1a, c1a)

    def stage_1b(k):
        s = lax.rem(k, 2)
        before_fill(k, h1b)
        for c, d in CD:
            h1a(k, c, d).wait_recv()
            take = piece(s, c, ring_at(pos1[c], 1 if d == 0 else SIDE - 1))
            s1b[s, c, d, pl.ds(2 * d, 2)] = (take(2 * d, 2) + r1a[s, c, d].astype(F32)).astype(BF16)
            s1b[s, c, d, pl.ds(2 - 2 * d, 2)] = take(2 - 2 * d, 2).astype(BF16)
        launch(k, h1b, c1b)
        give_credit(k, c1a, ring1)

    def stage_1c(k):
        s = lax.rem(k, 2)
        for c in range(2):
            for d in range(2):
                h1b(k, c, d).wait_recv()
            p1[s, c] = piece(s, c, pos1[c])(0, SIDE) + r1b[s, c, 0].astype(F32) + r1b[s, c, 1].astype(F32)
        give_credit(k, c1b, ring1)

    def stage_2a(k):
        s = lax.rem(k, 2)
        before_fill(k, h2a)
        for c, d in CD:
            s2a[s, c, d] = p1[s, c, ring_at(pos2[c], 2), pl.ds(d * hs, hs)].astype(BF16)
        launch(k, h2a, c2a)

    def stage_2b(k):
        s = lax.rem(k, 2)
        before_fill(k, h2b)
        for c, d in CD:
            h2a(k, c, d).wait_recv()
            q = ring_at(pos2[c], 1 if d == 0 else SIDE - 1)
            same, other = pl.ds(d * hs, hs), pl.ds((1 - d) * hs, hs)
            s2b[s, c, d, same] = (p1[s, c, q, same] + r2a[s, c, d].astype(F32)).astype(BF16)
            s2b[s, c, d, other] = p1[s, c, q, other].astype(BF16)
        launch(k, h2b, c2b)
        give_credit(k, c2a, ring2)

    def fin_copies(k):
        s = lax.rem(k, 2)
        return [
            (g, pltpu.make_async_copy(fin.at[s], o.at[k - g * per_group], fin_sem.at[s]))
            for g, o in enumerate(outs)
        ]

    def of_group(k, act):
        for g, copy in fin_copies(k):
            @pl.when((k >= g * per_group) & (k < (g + 1) * per_group))
            def _():
                act(copy)

    def stage_2c(k):
        s = lax.rem(k, 2)

        @pl.when(k >= 2)
        def _():
            of_group(k - 2, lambda copy: copy.wait())

        for c in range(2):
            for d in range(2):
                h2b(k, c, d).wait_recv()
            total = p1[s, c, pos2[c]] + r2b[s, c, 0].astype(F32) + r2b[s, c, 1].astype(F32)
            fin[s, c] = total.astype(BF16)
        of_group(k, lambda copy: copy.start())
        give_credit(k, c2b, ring2)

    def run(stage, k):
        @pl.when((k >= 0) & (k < nch))
        def _():
            stage(k)

    @pl.loop(0, nch + 4)
    def _(i):
        run(stage_a, i)
        run(stage_2b, i - 4)
        run(stage_b, i)
        run(stage_1c, i - 3)
        run(stage_2a, i - 3)
        run(stage_1b, i - 2)
        run(stage_c, i - 1)
        run(stage_1a, i - 1)
        run(stage_2c, i - 4)

    for k in (nch - 2, nch - 1):
        grads_copy(k).wait()
        for a in range(SIDE):
            pair_copy(k, a).wait_send()
        for h in (h1a, h1b, h2a, h2b):
            for c, d in CD:
                h(k, c, d).wait_send()
        g = k // per_group
        pltpu.make_async_copy(fin.at[k % 2], outs[g].at[k - g * per_group], fin_sem.at[k % 2]).wait()


def reduce_call(dy, gate, up, wg, wu, wd):
    rows, d = dy.shape
    f = wg.shape[1]
    nch = rows // R
    sub = d // (2 * SIDE * SIDE)
    quarter = sub * SIDE
    ANY = pl.BlockSpec(memory_space=pl.ANY)
    dma = pltpu.SemaphoreType.DMA
    return pl.pallas_call(
        functools.partial(reduce_kernel, nch),
        out_shape=[jax.ShapeDtypeStruct((3 * f, rows), BF16)]
        + [jax.ShapeDtypeStruct((nch // GROUPS, 2, sub, L), BF16)] * GROUPS,
        in_specs=[ANY] * 6,
        out_specs=[ANY] * (1 + GROUPS),
        scratch_shapes=[
            pltpu.VMEM((d, 2 * f), BF16),
            pltpu.VMEM((f, d), BF16),
            pltpu.VMEM((R, d), BF16),
            pltpu.VMEM((R, f), BF16),
            pltpu.VMEM((R, f), BF16),
            pltpu.VMEM((f, R), F32),
            pltpu.VMEM((2, 3 * f, R), BF16),
            pltpu.VMEM((2, SIDE, SIDE, sub, R), BF16),
            pltpu.VMEM((2, SIDE, SIDE, sub, R), BF16),
            pltpu.VMEM((2, SIDE, SIDE, sub, R), F32),
            pltpu.VMEM((2, 2, 2, 2, sub, L), BF16),
            pltpu.VMEM((2, 2, 2, 2, sub, L), BF16),
            pltpu.VMEM((2, 2, 2, SIDE, sub, L), BF16),
            pltpu.VMEM((2, 2, 2, SIDE, sub, L), BF16),
            pltpu.VMEM((2, 2, SIDE, sub, L), F32),
            pltpu.VMEM((2, 2, 2, sub // 2, L), BF16),
            pltpu.VMEM((2, 2, 2, sub // 2, L), BF16),
            pltpu.VMEM((2, 2, 2, sub, L), BF16),
            pltpu.VMEM((2, 2, 2, sub, L), BF16),
            pltpu.VMEM((2, 2, sub, L), BF16),
            dma((3,)),
            dma((3,)),
            dma((2,)),
            dma((2,)),
            dma((2, SIDE)),
            dma((2, SIDE)),
        ]
        + [dma((2, 2, 2))] * 8
        + [pltpu.SemaphoreType.REGULAR]
        + [pltpu.SemaphoreType.REGULAR((2, 2))] * 4,
        compiler_params=pltpu.CompilerParams(
            collective_id=0, has_side_effects=True, vmem_limit_bytes=VMEM_LIMIT
        ),
        cost_estimate=pl.CostEstimate(
            flops=6 * rows * d * f, bytes_accessed=2 * (rows * d + 3 * d * f), transcendentals=rows * f
        ),
        name="terms_reduce_scatter",
    )(dy, gate, up, wg, wu, wd)


def weights_kernel(x, dy, grads, dwg, dwu, dwd, done):
    f = dwd.shape[0]
    done[...] = jnp.zeros_like(done)
    for i, out in enumerate((dwg, dwu)):
        t = jnp.dot(grads[pl.ds(i * f, f)], x[...], preferred_element_type=F32)
        out[...] = t.T.astype(BF16)
    dwd[...] = jnp.dot(grads[pl.ds(2 * f, f)], dy[...], preferred_element_type=F32).astype(BF16)


def weights_call(x, dy, grads):
    rows, d = x.shape
    f = grads.shape[0] // 3
    n = min(512, d)
    return pl.pallas_call(
        weights_kernel,
        grid=(d // n,),
        out_shape=[
            jax.ShapeDtypeStruct((d, f), BF16),
            jax.ShapeDtypeStruct((d, f), BF16),
            jax.ShapeDtypeStruct((f, d), BF16),
            jax.ShapeDtypeStruct((8, 128), F32),
        ],
        in_specs=[
            pl.BlockSpec((rows, n), lambda j: (0, j)),
            pl.BlockSpec((rows, n), lambda j: (0, j)),
            pl.BlockSpec((3 * f, rows), lambda j: (0, 0), pipeline_mode=pl.Buffered(1)),
        ],
        out_specs=[
            pl.BlockSpec((n, f), lambda j: (j, 0)),
            pl.BlockSpec((n, f), lambda j: (j, 0)),
            pl.BlockSpec((f, n), lambda j: (0, j)),
            pl.BlockSpec((8, 128), lambda j: (0, 0)),
        ],
        compiler_params=pltpu.CompilerParams(vmem_limit_bytes=56 * 2**20),
        cost_estimate=pl.CostEstimate(
            flops=6 * rows * d * f, bytes_accessed=2 * (2 * rows * d + 3 * d * f), transcendentals=0
        ),
        name="weight_gradients",
    )(x, dy, grads)


def place_kernel(g, *refs):
    out = refs[-1]
    for c in range(2):
        stacked = jnp.concatenate([g[0, b, 0, 0, c] for b in range(SIDE)], axis=0)
        out[0, pl.ds(c * L, L)] = stacked.T


def place_call(g, gathered, into, nch, after):
    n, per_group, _, sub, _ = gathered.shape
    quarter = sub * SIDE
    d = quarter * SIDE * 2
    view = gathered.reshape(SIDE, SIDE, 2, per_group, 2, sub, L)
    ANY = pl.BlockSpec(memory_space=pl.ANY)
    extra = [into] if into is not None else []
    return pl.pallas_call(
        place_kernel,
        grid=(per_group, 2, SIDE),
        out_shape=jax.ShapeDtypeStruct((nch, R, d), BF16),
        in_specs=[
            pl.BlockSpec((1, SIDE, 1, 1, 2, sub, L), lambda k, c, a: (a, 0, c, k, 0, 0, 0)),
            ANY,
        ] + [ANY] * len(extra),
        out_specs=pl.BlockSpec((1, R, quarter), lambda k, c, a: (g * per_group + k, 0, c * SIDE + a)),
        input_output_aliases={2: 0} if extra else {},
        compiler_params=pltpu.CompilerParams(vmem_limit_bytes=32 * 2**20),
        cost_estimate=pl.CostEstimate(flops=n * per_group * sub * L * 200, bytes_accessed=8 * n * per_group * sub * L, transcendentals=0),
        name="place",
    )(view, after, *extra)


def solution(mesh):
    def step(x, dy, gate, up, w_gate, w_up, w_down):
        rows, d = x.shape
        nch = rows // R
        grads, *parts = reduce_call(dy, gate, up, w_gate, w_up, w_down)
        whole = [lax.all_gather(p, "tp", axis=0) for p in parts]
        dw_gate, dw_up, dw_down, done = weights_call(x, dy, grads)
        dx = None
        for g, part in enumerate(whole):
            dx = place_call(g, part, dx, nch, done)
        return dx.reshape(rows, d), dw_gate, dw_up, dw_down

    tokens, columns, rows = P("dp", None), P(None, "tp"), P("tp", None)
    return jax.shard_map(
        step,
        mesh=mesh,
        in_specs=(tokens, tokens, P("dp", "tp"), P("dp", "tp"), columns, columns, rows),
        out_specs=(tokens, P("dp", "tp"), P("dp", "tp"), P(("dp", "tp"), None)),
        check_vma=False,
    )
```

time: 356 us -> 292 us (0.82)
  Pallas kernels: 0 us -> 224 us
  matrix products: 192 us -> 0 us
  waiting for transfers between devices: 104 us -> 42.5 us
  local copies, waits for them, and re-layouts: 45.5 us -> 11 us
    pallas_call x0 -> x4, Pallas kernels: none -> 224 us  [the longest x1 127 us: reduce_call(): pl.pallas_call(functools.partial(reduce_kernel, nch), out_shape=[jax.Shap...]
    dot_general x6 -> x0, matrix products: 192 us -> none  [the longest x1 42.5 us: step(): jnp.dot(d_up, w_up.T, preferred_element_type=jnp.float32)]
    psum x1 -> x0, waiting for transfers between devices: 104 us -> none  [step(): dx = lax.psum(term.astype(jnp.bfloat16), 'tp')]
    all_gather x0 -> x2, waiting for transfers between devices: none -> 41.7 us  [step(): whole = [lax.all_gather(p, 'tp', axis=0) for p in parts]]
    unnamed x5 -> x8, local copies, waits for them, and re-layouts: 45.5 us -> 11 us
  transfers between devices with their start and end apart: 1 -> 2, of which waited for: 1 -> 1; matrix products, arithmetic and copies ran while one was open for 31% -> 0% of each run, Pallas kernels for 0% -> 28%
where the time goes in v1:
time: 292 us; the launch traced here: 291 us
  Pallas kernels  224 us (77%)
  waiting for transfers between devices  42.5 us (15%)
  between operations  14.1 us (5%)
  local copies, waits for them, and re-layouts  11 us (4%)
    pallas_call x1, Pallas kernels, reduce_call(): pl.pallas_call(functools.partial(reduce_kernel, nch), out_shape=[jax.Shap...  127 us
    pallas_call x1, Pallas kernels, weights_call(): pl.pallas_call(weights_kernel, grid=(d // n,), out_shape=[jax.ShapeDtypeS...  65 us
    all_gather x2, waiting for transfers between devices, step(): whole = [lax.all_gather(p, 'tp', axis=0) for p in parts]  41.7 us
    pallas_call x2, Pallas kernels, place_call(): pl.pallas_call(place_kernel, grid=(per_group, 2, SIDE), out_shape=jax.Sha...  31.5 us
    unnamed x8, local copies, waits for them, and re-layouts  11 us
  transfers between devices with their start and end apart: 2, of which 1 were waited for; matrix products, arithmetic and copies ran while one was open for 0% of the time, Pallas kernels for 28%

profile of v1, /device:TPU:97, one launch (start us, length us, event | category | flops | bytes accessed | tf_op | source)
XLA Modules:
  0.0 291.3 jit_solution(4486474460965012960)
XLA Ops:
  7.2 0.1 all-gather.7.cloned.1.call-start
  7.2 127.1 %terms_reduce_scatter.1 = (bf16[1920,2048]{1,0:T(8,128)(2,1)}, bf16[4,2,224,128]{3,2,1,0:T(8,128)(2,1)}, bf16[4,2,224,128]{3,2,1,0:T(8,128)(2,1)}) custom-call(bf16[2048,7168]{1,0:T(8,128)(2,1)} %dy.3, bf16[2048,640]{1,0:T(8,128)(2,1)} %gate.1, bf16[2048,640]{1,0:T(8,128)(2,1)} %up.1, bf16[7168,640]{1,0:T(8,128)(2,1)} %wg.1, bf16[7168,640]{1,0:T(8,128)(2,1)} %wu.1, ...), custom_call_target="tpu_custom_call" | custom-call | flops 56371445760 | bytes 56885248 | tf_op jit(solution)/shard_map/terms_reduce_scatter/pallas_call | solution.py:315
  134.3 0.1 all-gather.7.cloned.1.call-update
  134.4 0.1 all-gather.5.cloned.1.call-start
  134.4 0.7 all-gather.5.cloned.1.call-update
  135.2 65.0 %weight_gradients.1 = (bf16[7168,640]{1,0:T(8,128)(2,1)}, bf16[7168,640]{1,0:T(8,128)(2,1)}, bf16[640,7168]{1,0:T(8,128)(2,1)}, f32[8,128]{1,0:T(8,128)}) custom-call(bf16[2048,7168]{1,0:T(8,128)(2,1)} %x.1, bf16[2048,7168]{1,0:T(8,128)(2,1)} %dy.3, bf16[1920,2048]{1,0:T(8,128)(2,1)} %get-tuple-element.12.grads), custom_call_target="tpu_custom_call" | custom-call | flops 56371445760 | bytes 86245376 | tf_op jit(solution)/shard_map/weight_gradients/pallas_call | solution.py:375
  200.2 0.0 all-gather.7.cloned.1.call-done
  200.2 0.0 copy-start.1
  200.2 5.2 %copy-done.1 = bf16[128,2,224,128]{3,2,1,0:T(8,128)(2,1)S(1)} copy-done((bf16[128,2,224,128]{3,2,1,0:T(8,128)(2,1)S(1)}, bf16[128,2,224,128]{3,2,1,0:T(8,128)(2,1)}, u32[]{:S(2)}) %copy-start.1) | copy-done | bytes 14680088
  205.4 0.0 copy-start.2
  205.4 0.7 copy-done.2
  206.1 0.0 copy-start.3
  206.1 15.8 %place.2.refs_1_ = bf16[8,256,7168]{2,1,0:T(8,128)(2,1)} custom-call(bf16[4,4,2,4,2,224,128]{6,5,4,3,2,1,0:T(8,128)(2,1)S(1)} %bitcast.4, f32[8,128]{1,0:T(8,128)S(1)} %copy-done.2), custom_call_target="tpu_custom_call" | custom-call | flops 734003200 | bytes 29360128 | tf_op jit(solution)/shard_map/place/pallas_call | solution.py:417
  221.8 41.7 %all-gather.5.cloned.1.call-done = bf16[128,2,224,128]{3,2,1,0:T(8,128)(2,1)} async-done(((bf16[4,2,224,128]{3,2,1,0:T(8,128)(2,1)}), bf16[128,2,224,128]{3,2,1,0:T(8,128)(2,1)}) %all-gather.5.cloned.1.call-update) | async-done | bytes 14680080 | tf_op jit(solution)/shard_map/all_gather | solution.py:438
  263.5 0.0 copy-done.3
  263.5 0.0 copy-start
  263.5 5.2 %copy-done = bf16[128,2,224,128]{3,2,1,0:T(8,128)(2,1)S(1)} copy-done((bf16[128,2,224,128]{3,2,1,0:T(8,128)(2,1)S(1)}, bf16[128,2,224,128]{3,2,1,0:T(8,128)(2,1)}, u32[]{:S(2)}) %copy-start) | copy-done | bytes 14680088
  268.7 15.8 %place.3 = bf16[8,256,7168]{2,1,0:T(8,128)(2,1)} custom-call(bf16[4,4,2,4,2,224,128]{6,5,4,3,2,1,0:T(8,128)(2,1)S(1)} %bitcast.3, f32[8,128]{1,0:T(8,128)S(1)} %copy-done.3, bf16[8,256,7168]{2,1,0:T(8,128)(2,1)} %place.2.refs_1_), custom_call_target="tpu_custom_call", output_to_operand_aliasing={{}: (2, {})} | custom-call | flops 734003200 | bytes 29360128 | tf_op jit(solution)/shard_map/place/pallas_call | solution.py:417
Async XLA Ops:
  7.2 193.1 %all-gather.7.cloned.1.call-start = ((), (), s32[]{:S(2)}) async-start(), calls=%async_computation.1 | async-start | bytes 15138816 | tf_op jit(solution)/shard_map/all_gather | solution.py:438
  134.4 129.2 %all-gather.5.cloned.1.call-start = ((), (), s32[]{:S(2)}) async-start(), calls=%async_computation | async-start | bytes 15138816 | tf_op jit(solution)/shard_map/all_gather | solution.py:438
  200.2 5.2 %copy-start.1 = (bf16[128,2,224,128]{3,2,1,0:T(8,128)(2,1)S(1)}, bf16[128,2,224,128]{3,2,1,0:T(8,128)(2,1)}, u32[]{:S(2)}) copy-start(bf16[128,2,224,128]{3,2,1,0:T(8,128)(2,1)} %all-gather.7.cloned.1.call-done) | copy-start | bytes 44040196
  205.4 0.7 copy-start.2
  206.1 57.5 %copy-start.3 = (f32[8,128]{1,0:T(8,128)S(1)}, f32[8,128]{1,0:T(8,128)}, u32[]{:S(2)}) copy-start(f32[8,128]{1,0:T(8,128)} %get-tuple-element.13.refs_0_) | copy-start | bytes 12292
  263.5 5.2 %copy-start = (bf16[128,2,224,128]{3,2,1,0:T(8,128)(2,1)S(1)}, bf16[128,2,224,128]{3,2,1,0:T(8,128)(2,1)}, u32[]{:S(2)}) copy-start(bf16[128,2,224,128]{3,2,1,0:T(8,128)(2,1)} %all-gather.5.cloned.1.call-done) | copy-start | bytes 44040196
Sparse Core Ops, SparseCore 0:
  134.5 65.0 all-gather.6
  201.7 61.7 all-gather.4

commit v2 on v1

v2 whole, which is shorter than its diff:
```python
import functools

import jax
import jax.numpy as jnp
from jax import lax
from jax.experimental import pallas as pl
from jax.experimental.pallas import tpu as pltpu
from jax.sharding import PartitionSpec as P

MESH = pl.DeviceIdType.MESH
BF16, F32 = jnp.bfloat16, jnp.float32
R = 256
L = 128
SIDE = 4
N = 256
O3A, O3B, O4A, O4B, O5 = 4, 5, 6, 8, 9
NT = (((1,), (1,)), ((), ()))
VMEM_LIMIT = 66_900_000


def block_kernel(
    nch, x_in, dy, gate, up, wg, wu, wd, grads, whole, dwg, dwu, dwd,
    dyv, gv, uv, dh, dt, obuf, pbuf, cs, s1a, r1a, s1b, r1b, p1, s2a, r2a, s2b, r2b, fin,
    in_sem, w_sem, dt_sem, fin_sem, ps, pr, ss1a, sr1a, ss1b, sr1b, ss2a, sr2a, ss2b, sr2b,
    ss3a, sr3a, ss3b, sr3b, ss4a, sr4a, ss4b, sr4b, ss5, sr5, g_sem, x_sem, o_sem,
    cp, c1a, c1b, c2a, c2b,
):
    f = wg.shape[1]
    half = wg.shape[0] // 2
    quarter = half // SIDE
    sub = quarter // SIDE
    hs = sub // 2

    me = lax.axis_index("tp")
    core = lax.rem(me, 2)
    y = lax.rem(me // 2, SIDE)
    x = me // (2 * SIDE)

    def at(i, j, c):
        return (lax.rem(i + SIDE, SIDE) * SIDE + lax.rem(j + SIDE, SIDE)) * 2 + c

    partner = at(x, y, 1 - core)
    xn = (at(x + 1, y, core), at(x - 1, y, core))
    yn = (at(x, y + 1, core), at(x, y - 1, core))
    ring1, pos1 = (xn, yn), (x, y)
    ring2, pos2 = (yn, xn), (y, x)

    def fetch(k):
        rows = pl.ds(pl.multiple_of(k * R, R), R)
        return [
            pltpu.make_async_copy(dy.at[rows], dyv, in_sem.at[0]),
            pltpu.make_async_copy(gate.at[rows], gv, in_sem.at[1]),
            pltpu.make_async_copy(up.at[rows], uv, in_sem.at[2]),
        ]

    def weight_copies(w, wdv):
        return [
            pltpu.make_async_copy(wd, wdv, w_sem.at[0]),
            pltpu.make_async_copy(wg, w.at[:, pl.ds(0, f)], w_sem.at[1]),
            pltpu.make_async_copy(wu, w.at[:, pl.ds(f, f)], w_sem.at[2]),
        ]

    def remote(src, dst, ssem, rsem, dev):
        return pltpu.make_async_remote_copy(
            src_ref=src, dst_ref=dst, send_sem=ssem, recv_sem=rsem,
            device_id={"tp": dev}, device_id_type=MESH,
        )

    def pair_copy(k, a):
        s = lax.rem(k, 2)
        return remote(obuf.at[s, a], pbuf.at[s, a], ps.at[s, a], pr.at[s, a], partner)

    def hop(k, c, d, src, dst, ssem, rsem, ring):
        s = lax.rem(k, 2)
        return remote(src.at[s, c, d], dst.at[s, c, d], ssem.at[s, c, d], rsem.at[s, c, d], ring[c][d])

    h1a = lambda k, c, d: hop(k, c, d, s1a, r1a, ss1a, sr1a, ring1)
    h1b = lambda k, c, d: hop(k, c, d, s1b, r1b, ss1b, sr1b, ring1)
    h2a = lambda k, c, d: hop(k, c, d, s2a, r2a, ss2a, sr2a, ring2)
    h2b = lambda k, c, d: hop(k, c, d, s2b, r2b, ss2b, sr2b, ring2)
    CD = [(c, d) for c in range(2) for d in range(2)]

    def before_fill(k, h):
        @pl.when(k >= 2)
        def _():
            for c, d in CD:
                h(k - 2, c, d).wait_send()

    def launch(k, h, credit):
        @pl.when(k >= 2)
        def _():
            for c, d in CD:
                pl.semaphore_wait(credit.at[c, d], 1)
        for c, d in CD:
            h(k, c, d).start()

    def give_credit(k, credit, ring):
        @pl.when(k + 2 < nch)
        def _():
            for c, d in CD:
                pl.semaphore_signal(
                    credit.at[c, d], inc=1, device_id={"tp": ring[c][1 - d]}, device_id_type=MESH
                )

    def ring_at(p, off):
        return lax.rem(p + off, SIDE)

    def piece(s, c, q):
        if c == 0:
            return lambda lo, n: cs[s, q, pl.ds(lo, n), :, pl.ds(0, L)]
        return lambda lo, n: cs[s, pl.ds(lo, n), q, :, pl.ds(L, L)]

    def grads_copy(k):
        s = lax.rem(k, 2)
        return pltpu.make_async_copy(
            dt.at[s], grads.at[:, pl.ds(pl.multiple_of(k * R, R), R)], dt_sem.at[s]
        )

    def stage_a(w, wdv, k):
        s = lax.rem(k, 2)
        for c in fetch(k):
            c.wait()

        @pl.when(k == 0)
        def _():
            weight_copies(w, wdv)[0].wait()

        depth = dyv.shape[1] // 4
        dh[...] = jnp.zeros_like(dh)

        @pl.loop(0, 4)
        def _(j):
            cols = pl.ds(pl.multiple_of(j * depth, depth), depth)
            dh[...] += lax.dot_general(wdv[:, cols], dyv[:, cols], NT, preferred_element_type=F32)

        @pl.when(k >= 2)
        def _():
            grads_copy(k - 2).wait()

        g = gv[...].astype(F32).T
        u = uv[...].astype(F32).T
        d = dh[...]
        sig = 1.0 / (1.0 + jnp.exp(-g))
        silu = g * sig
        dt[s, pl.ds(2 * f, f)] = (silu * u).astype(BF16)
        dt[s, pl.ds(f, f)] = (d * silu).astype(BF16)
        dt[s, pl.ds(0, f)] = (d * u * (sig + silu * (1.0 - sig))).astype(BF16)
        grads_copy(k).start()

        @pl.when(k + 1 < nch)
        def _():
            for c in fetch(k + 1):
                c.start()

    def rows_of(h, a):
        return pl.ds(pl.multiple_of(h * half + a * quarter, quarter), quarter)

    def stage_b(w, wdv, k):
        s = lax.rem(k, 2)

        @pl.when(k == 0)
        def _():
            for copy in weight_copies(w, wdv)[1:]:
                copy.wait()

        @pl.when(k >= 2)
        def _():
            pl.semaphore_wait(cp, 1)

        @pl.loop(0, SIDE)
        def _(a):
            @pl.when(k >= 2)
            def _():
                pair_copy(k - 2, a).wait_send()

            t = jnp.dot(w[rows_of(1 - core, a)], dt[s, pl.ds(0, 2 * f)], preferred_element_type=F32)
            obuf[s, a] = t.astype(BF16).reshape(SIDE, sub, R)
            pair_copy(k, a).start()

    def stage_c(w, wdv, k):
        s = lax.rem(k, 2)

        @pl.loop(0, SIDE)
        def _(a):
            t = jnp.dot(w[rows_of(core, a)], dt[s, pl.ds(0, 2 * f)], preferred_element_type=F32)
            pair_copy(k, a).wait_recv()
            cs[s, a] = t.reshape(SIDE, sub, R) + pbuf[s, a].astype(F32)

        @pl.when(k + 2 < nch)
        def _():
            pl.semaphore_signal(cp, inc=1, device_id={"tp": partner}, device_id_type=MESH)

    def stage_1a(k):
        s = lax.rem(k, 2)
        before_fill(k, h1a)
        for c in range(2):
            take = piece(s, c, ring_at(pos1[c], 2))
            for d in range(2):
                s1a[s, c, d] = take(2 * d, 2).astype(BF16)
        launch(k, h1a, c1a)

    def stage_1b(k):
        s = lax.rem(k, 2)
        before_fill(k, h1b)
        for c, d in CD:
            h1a(k, c, d).wait_recv()
            take = piece(s, c, ring_at(pos1[c], 1 if d == 0 else SIDE - 1))
            s1b[s, c, d, pl.ds(2 * d, 2)] = (take(2 * d, 2) + r1a[s, c, d].astype(F32)).astype(BF16)
            s1b[s, c, d, pl.ds(2 - 2 * d, 2)] = take(2 - 2 * d, 2).astype(BF16)
        launch(k, h1b, c1b)
        give_credit(k, c1a, ring1)

    def stage_1c(k):
        s = lax.rem(k, 2)
        for c in range(2):
            for d in range(2):
                h1b(k, c, d).wait_recv()
            p1[s, c] = piece(s, c, pos1[c])(0, SIDE) + r1b[s, c, 0].astype(F32) + r1b[s, c, 1].astype(F32)
        give_credit(k, c1b, ring1)

    def stage_2a(k):
        s = lax.rem(k, 2)
        before_fill(k, h2a)
        for c, d in CD:
            s2a[s, c, d] = p1[s, c, ring_at(pos2[c], 2), pl.ds(d * hs, hs)].astype(BF16)
        launch(k, h2a, c2a)

    def stage_2b(k):
        s = lax.rem(k, 2)
        before_fill(k, h2b)
        for c, d in CD:
            h2a(k, c, d).wait_recv()
            q = ring_at(pos2[c], 1 if d == 0 else SIDE - 1)
            same, other = pl.ds(d * hs, hs), pl.ds((1 - d) * hs, hs)
            s2b[s, c, d, same] = (p1[s, c, q, same] + r2a[s, c, d].astype(F32)).astype(BF16)
            s2b[s, c, d, other] = p1[s, c, q, other].astype(BF16)
        launch(k, h2b, c2b)
        give_credit(k, c2a, ring2)

    def stage_2c(k):
        s = lax.rem(k, 2)
        for c in range(2):
            for d in range(2):
                h2b(k, c, d).wait_recv()
            total = p1[s, c, pos2[c]] + r2b[s, c, 0].astype(F32) + r2b[s, c, 1].astype(F32)
            fin[k, c] = total.astype(BF16)
        give_credit(k, c2b, ring2)

    def own_copy(k, c):
        return pltpu.make_async_copy(fin.at[k, c], whole.at[k, core, c, pos1[c], pos2[c]], fin_sem.at[k, c])

    def spread(k, c, d, src, dst, ssem, rsem, ring):
        return remote(src, dst, ssem.at[k, c, d], rsem.at[k, c, d], ring[c][d])

    def came_from(p, d):
        return ring_at(p, SIDE - 1 if d == 0 else 1)

    def h3a(k, c, d):
        dst = whole.at[k, core, c, pos1[c], pos2[c]]
        return spread(k, c, d, fin.at[k, c], dst, ss3a, sr3a, ring2)

    def h3b(k, c, d):
        at3 = whole.at[k, core, c, pos1[c], came_from(pos2[c], d), pl.ds(d * hs, hs)]
        return spread(k, c, d, at3, at3, ss3b, sr3b, ring2)

    def h4a(k, c, d):
        at4 = whole.at[k, core, c, pos1[c]]
        return spread(k, c, d, at4, at4, ss4a, sr4a, ring1)

    def h4b(k, c, d):
        at4 = whole.at[k, core, c, came_from(pos1[c], d), pl.ds(2 * d, 2)]
        return spread(k, c, d, at4, at4, ss4b, sr4b, ring1)

    def h5(k, c):
        at5 = whole.at[k, core, c]
        return remote(at5, at5, ss5.at[k, c], sr5.at[k, c], partner)

    def stage_3a(k):
        for c in range(2):
            own_copy(k, c).start()
        for c, d in CD:
            h3a(k, c, d).start()

    def stage_3b(k):
        for c, d in CD:
            h3a(k, c, d).wait_recv()
            h3b(k, c, d).start()

    def stage_4a(k):
        for c in range(2):
            own_copy(k, c).wait()
            for d in range(2):
                h3b(k, c, d).wait_recv()
            for d in range(2):
                h4a(k, c, d).start()

    def stage_4b(k):
        for c, d in CD:
            h4a(k, c, d).wait_recv()
            h4b(k, c, d).start()

    def stage_5(k):
        for c in range(2):
            for d in range(2):
                h4b(k, c, d).wait_recv()
            h5(k, c).start()

    def run(stage, k):
        @pl.when((k >= 0) & (k < nch))
        def _():
            stage(k)

    def terms(w, wdv):
        copies = weight_copies(w, wdv)
        first = fetch(0)
        first[0].start()
        copies[0].start()
        first[1].start()
        first[2].start()
        copies[1].start()
        copies[2].start()

        barrier = pltpu.get_barrier_semaphore()
        for peer in (partner, *xn, *yn):
            pl.semaphore_signal(barrier, inc=1, device_id={"tp": peer}, device_id_type=MESH)
        pl.semaphore_wait(barrier, 5)

        @pl.loop(0, nch + 1)
        def _(i):
            run(functools.partial(stage_a, w, wdv), i)
            run(stage_2b, i - 4)
            run(functools.partial(stage_b, w, wdv), i)
            run(stage_1c, i - 3)
            run(stage_2a, i - 3)
            run(stage_1b, i - 2)
            run(functools.partial(stage_c, w, wdv), i - 1)
            run(stage_1a, i - 1)
            run(stage_2c, i - 4)
            run(stage_3a, i - O3A)
            run(stage_3b, i - O3B)
            run(stage_4a, i - O4A)
            run(stage_4b, i - O4B)
            run(stage_5, i - O5)

    pl.run_scoped(terms, pltpu.VMEM((2 * half, 2 * f), BF16), pltpu.VMEM((f, 2 * half), BF16))

    for k in (nch - 2, nch - 1):
        grads_copy(k).wait()

    blocks = 2 * half // N
    tail = nch + O5
    per_step = -(-blocks // (tail - nch - 1))

    def weights(gr, xv, dv, gst, dst):
        load = pltpu.make_async_copy(grads, gr, g_sem)

        def cols(j):
            return pl.ds(pl.multiple_of(j * N, N), N)

        def ins(j):
            s = lax.rem(j, 2)
            return [
                pltpu.make_async_copy(x_in.at[:, cols(j)], xv.at[s], x_sem.at[s, 0]),
                pltpu.make_async_copy(dy.at[:, cols(j)], dv.at[s], x_sem.at[s, 1]),
            ]

        def results(j):
            s = lax.rem(j, 2)
            return [
                pltpu.make_async_copy(gst.at[s, 0], dwg.at[cols(j)], o_sem.at[s, 0]),
                pltpu.make_async_copy(gst.at[s, 1], dwu.at[cols(j)], o_sem.at[s, 1]),
                pltpu.make_async_copy(dst.at[s], dwd.at[:, cols(j)], o_sem.at[s, 2]),
            ]

        def unit(j):
            s = lax.rem(j, 2)

            @pl.when(j == 0)
            def _():
                load.wait()

            for copy in ins(j):
                copy.wait()

            @pl.when(j >= 2)
            def _():
                for copy in results(j - 2):
                    copy.wait()

            for m in range(2):
                t = jnp.dot(gr[pl.ds(m * f, f)], xv[s], preferred_element_type=F32)
                gst[s, m] = t.T.astype(BF16)
            dst[s] = jnp.dot(gr[pl.ds(2 * f, f)], dv[s], preferred_element_type=F32).astype(BF16)
            for copy in results(j):
                copy.start()

            @pl.when(j + 2 < blocks)
            def _():
                for copy in ins(j + 2):
                    copy.start()

        def units(lo, hi):
            @pl.loop(lo, hi)
            def _(j):
                @pl.when(j < blocks)
                def _():
                    unit(j)

        load.start()
        for j in (0, 1):
            for copy in ins(j):
                copy.start()

        split = per_step // 2

        @pl.loop(nch + 1, tail)
        def _(i):
            j = (i - nch - 1) * per_step
            run(stage_2b, i - 4)
            run(stage_1c, i - 3)
            run(stage_2a, i - 3)
            run(stage_1b, i - 2)
            units(j, j + split)
            run(stage_2c, i - 4)
            run(stage_3a, i - O3A)
            run(stage_3b, i - O3B)
            units(j + split, j + per_step)
            run(stage_4a, i - O4A)
            run(stage_4b, i - O4B)
            run(stage_5, i - O5)

        for j in (blocks - 2, blocks - 1):
            for copy in results(j):
                copy.wait()

    pl.run_scoped(
        weights,
        pltpu.VMEM((3 * f, nch * R), BF16),
        pltpu.VMEM((2, nch * R, N), BF16),
        pltpu.VMEM((2, nch * R, N), BF16),
        pltpu.VMEM((2, 2, N, f), BF16),
        pltpu.VMEM((2, f, N), BF16),
    )

    for k in (nch - 2, nch - 1):
        for a in range(SIDE):
            pair_copy(k, a).wait_send()
        for h in (h1a, h1b, h2a, h2b):
            for c, d in CD:
                h(k, c, d).wait_send()

    @pl.loop(0, nch)
    def _(k):
        for h in (h3a, h3b, h4a, h4b):
            for c, d in CD:
                h(k, c, d).wait_send()
        for c in range(2):
            h5(k, c).wait()


def block_call(x, dy, gate, up, wg, wu, wd):
    rows, d = dy.shape
    f = wg.shape[1]
    nch = rows // R
    sub = d // (2 * SIDE * SIDE)
    ANY = pl.BlockSpec(memory_space=pl.ANY)
    dma = pltpu.SemaphoreType.DMA
    return pl.pallas_call(
        functools.partial(block_kernel, nch),
        out_shape=[
            jax.ShapeDtypeStruct((3 * f, rows), BF16),
            jax.ShapeDtypeStruct((nch, 2, 2, SIDE, SIDE, sub, L), BF16),
            jax.ShapeDtypeStruct((d, f), BF16),
            jax.ShapeDtypeStruct((d, f), BF16),
            jax.ShapeDtypeStruct((f, d), BF16),
        ],
        in_specs=[ANY] * 7,
        out_specs=[ANY] * 5,
        scratch_shapes=[
            pltpu.VMEM((R, d), BF16),
            pltpu.VMEM((R, f), BF16),
            pltpu.VMEM((R, f), BF16),
            pltpu.VMEM((f, R), F32),
            pltpu.VMEM((2, 3 * f, R), BF16),
            pltpu.VMEM((2, SIDE, SIDE, sub, R), BF16),
            pltpu.VMEM((2, SIDE, SIDE, sub, R), BF16),
            pltpu.VMEM((2, SIDE, SIDE, sub, R), F32),
            pltpu.VMEM((2, 2, 2, 2, sub, L), BF16),
            pltpu.VMEM((2, 2, 2, 2, sub, L), BF16),
            pltpu.VMEM((2, 2, 2, SIDE, sub, L), BF16),
            pltpu.VMEM((2, 2, 2, SIDE, sub, L), BF16),
            pltpu.VMEM((2, 2, SIDE, sub, L), F32),
            pltpu.VMEM((2, 2, 2, sub // 2, L), BF16),
            pltpu.VMEM((2, 2, 2, sub // 2, L), BF16),
            pltpu.VMEM((2, 2, 2, sub, L), BF16),
            pltpu.VMEM((2, 2, 2, sub, L), BF16),
            pltpu.VMEM((nch, 2, sub, L), BF16),
            dma((3,)),
            dma((3,)),
            dma((2,)),
            dma((nch, 2)),
            dma((2, SIDE)),
            dma((2, SIDE)),
        ]
        + [dma((2, 2, 2))] * 8
        + [dma((nch, 2, 2))] * 8
        + [dma((nch, 2))] * 2
        + [dma, dma((2, 2)), dma((2, 3))]
        + [pltpu.SemaphoreType.REGULAR]
        + [pltpu.SemaphoreType.REGULAR((2, 2))] * 4,
        compiler_params=pltpu.CompilerParams(
            collective_id=0, has_side_effects=True, vmem_limit_bytes=VMEM_LIMIT
        ),
        cost_estimate=pl.CostEstimate(
            flops=12 * rows * d * f, bytes_accessed=8 * rows * d + 12 * d * f, transcendentals=rows * f
        ),
        name="mlp_backward",
    )(x, dy, gate, up, wg, wu, wd)


def place_kernel(g, out):
    for c in range(2):
        for a in range(SIDE):
            pieces = [g[0, 0, c, a, b] if c == 0 else g[0, 0, c, b, a] for b in range(SIDE)]
            stacked = jnp.concatenate(pieces, axis=0)
            n = stacked.shape[0]
            out[0, pl.ds(c * L, L), pl.ds(a * n, n)] = stacked.T


def place_call(whole):
    nch, _, _, _, _, sub, _ = whole.shape
    half = sub * SIDE * SIDE
    return pl.pallas_call(
        place_kernel,
        grid=(nch, 2),
        out_shape=jax.ShapeDtypeStruct((nch, R, 2 * half), BF16),
        in_specs=[pl.BlockSpec((1, 1, 2, SIDE, SIDE, sub, L), lambda k, c: (k, c, 0, 0, 0, 0, 0))],
        out_specs=pl.BlockSpec((1, R, half), lambda k, c: (k, 0, c)),
        compiler_params=pltpu.CompilerParams(vmem_limit_bytes=60 * 2**20),
        cost_estimate=pl.CostEstimate(
            flops=nch * R * half * 64, bytes_accessed=8 * nch * R * half, transcendentals=0
        ),
        name="place",
    )(whole)


def solution(mesh):
    def step(x, dy, gate, up, w_gate, w_up, w_down):
        _, whole, dw_gate, dw_up, dw_down = block_call(x, dy, gate, up, w_gate, w_up, w_down)
        return place_call(whole).reshape(x.shape), dw_gate, dw_up, dw_down

    tokens, columns, rows = P("dp", None), P(None, "tp"), P("tp", None)
    return jax.shard_map(
        step,
        mesh=mesh,
        in_specs=(tokens, tokens, P("dp", "tp"), P("dp", "tp"), columns, columns, rows),
        out_specs=(tokens, P("dp", "tp"), P("dp", "tp"), P(("dp", "tp"), None)),
        check_vma=False,
    )
```

time: 292 us -> 273 us (0.935)
  waiting for transfers between devices: 42.5 us -> 0 us
  Pallas kernels: 224 us -> 248 us
  between operations: 14.1 us -> 0.64 us
  local copies, waits for them, and re-layouts: 11 us -> 23.9 us
    all_gather x2 -> x0, waiting for transfers between devices: 41.7 us -> none  [step(): whole = [lax.all_gather(p, 'tp', axis=0) for p in parts]]
    pallas_call x4 -> x2, Pallas kernels: 224 us -> 248 us  [the longest x1 221 us: block_call(): pl.pallas_call(functools.partial(block_kernel, nch), out_shape=[jax.Shape...]
    unnamed x8 -> x3, local copies, waits for them, and re-layouts: 11 us -> 23.9 us
  transfers between devices with their start and end apart: 2 -> 0, of which waited for: 1 -> 0; matrix products, arithmetic and copies ran while one was open for 0% -> 0% of each run, Pallas kernels for 28% -> 0%
where the time goes in v2:
time: 273 us
  Pallas kernels  248 us (91%)
  local copies, waits for them, and re-layouts  23.9 us (9%)
    pallas_call x1, Pallas kernels, block_call(): pl.pallas_call(functools.partial(block_kernel, nch), out_shape=[jax.Shape...  221 us
    pallas_call x1, Pallas kernels, place_call(): pl.pallas_call(place_kernel, grid=(nch, 2), out_shape=jax.ShapeDtypeStruc...  27.4 us
    unnamed x3, local copies, waits for them, and re-layouts  23.9 us

profile of v2, /device:TPU:97, one launch (start us, length us, event | category | flops | bytes accessed | tf_op | source)
XLA Modules:
  0.0 272.8 jit_solution(4431570788392881988)
XLA Ops:
  0.6 220.8 %mlp_backward.1 = (bf16[1920,2048]{1,0:T(8,128)(2,1)}, bf16[8,2,2,4,4,224,128]{6,5,4,3,2,1,0:T(8,128)(2,1)}, bf16[7168,640]{1,0:T(8,128)(2,1)}, bf16[7168,640]{1,0:T(8,128)(2,1)}, bf16[640,7168]{1,0:T(8,128)(2,1)}) custom-call(bf16[2048,7168]{1,0:T(8,128)(2,1)} %x_in.1, bf16[2048,7168]{1,0:T(8,128)(2,1)} %dy.1, bf16[2048,640]{1,0:T(8,128)(2,1)} %gate.1, ...), custom_call_target="tpu_custom_call" | custom-call | flops 112742891520 | bytes 172490752 | tf_op jit(solution)/shard_map/mlp_backward/pallas_call | solution.py:468
  221.5 27.4 %place.1 = bf16[8,256,7168]{2,1,0:T(8,128)(2,1)} custom-call(bf16[8,2,2,4,4,224,128]{6,5,4,3,2,1,0:T(8,128)(2,1)} %get-tuple-element.8.g), custom_call_target="tpu_custom_call" | custom-call | flops 469762048 | bytes 58720256 | tf_op jit(solution)/shard_map/place/pallas_call | solution.py:533
  248.9 8.0 %copy.14 = bf16[7168,640]{1,0:T(8,128)(2,1)} copy(bf16[7168,640]{1,0:T(8,128)(2,1)} %get-tuple-element.17) | data formatting | bytes 18350080
  256.9 8.0 %copy.15 = bf16[7168,640]{1,0:T(8,128)(2,1)} copy(bf16[7168,640]{1,0:T(8,128)(2,1)} %get-tuple-element.18) | data formatting | bytes 18350080
  265.0 7.9 %copy.16 = bf16[640,7168]{1,0:T(8,128)(2,1)} copy(bf16[640,7168]{1,0:T(8,128)(2,1)} %get-tuple-element.19) | data formatting | bytes 18350080

commit v3 on v2

--- a/solution.py
+++ b/solution.py
@@ -13,7 +13,7 @@
 L = 128
 SIDE = 4
 N = 256
-O3A, O3B, O4A, O4B, O5 = 4, 5, 6, 8, 9
+O3A, O3B, O4A, O4B, O5 = 6, 7, 8, 9, 10
 NT = (((1,), (1,)), ((), ()))
 VMEM_LIMIT = 66_900_000
 
@@ -54,11 +54,16 @@
         ]
 
     def weight_copies(w, wdv):
-        return [
-            pltpu.make_async_copy(wd, wdv, w_sem.at[0]),
-            pltpu.make_async_copy(wg, w.at[:, pl.ds(0, f)], w_sem.at[1]),
-            pltpu.make_async_copy(wu, w.at[:, pl.ds(f, f)], w_sem.at[2]),
-        ]
+        copies = [pltpu.make_async_copy(wd, wdv, w_sem.at[0])]
+        for i, h in enumerate((1 - core, core)):
+            rows = pl.ds(pl.multiple_of(h * half, half), half)
+            for m, source in enumerate((wg, wu)):
+                copies.append(
+                    pltpu.make_async_copy(
+                        source.at[rows], w.at[rows, pl.ds(m * f, f)], w_sem.at[1 + 2 * i + m]
+                    )
+                )
+        return copies
 
     def remote(src, dst, ssem, rsem, dev):
         return pltpu.make_async_remote_copy(
@@ -160,7 +165,7 @@
 
         @pl.when(k == 0)
         def _():
-            for copy in weight_copies(w, wdv)[1:]:
+            for copy in weight_copies(w, wdv)[1:3]:
                 copy.wait()
 
         @pl.when(k >= 2)
@@ -179,6 +184,11 @@
 
     def stage_c(w, wdv, k):
         s = lax.rem(k, 2)
+
+        @pl.when(k == 0)
+        def _():
+            for copy in weight_copies(w, wdv)[3:]:
+                copy.wait()
 
         @pl.loop(0, SIDE)
         def _(a):
@@ -317,25 +327,25 @@
         copies[0].start()
         first[1].start()
         first[2].start()
-        copies[1].start()
-        copies[2].start()
+        for copy in copies[1:]:
+            copy.start()
 
         barrier = pltpu.get_barrier_semaphore()
         for peer in (partner, *xn, *yn):
             pl.semaphore_signal(barrier, inc=1, device_id={"tp": peer}, device_id_type=MESH)
         pl.semaphore_wait(barrier, 5)
 
-        @pl.loop(0, nch + 1)
+        @pl.loop(0, nch)
         def _(i):
-            run(functools.partial(stage_a, w, wdv), i)
-            run(stage_2b, i - 4)
-            run(functools.partial(stage_b, w, wdv), i)
-            run(stage_1c, i - 3)
-            run(stage_2a, i - 3)
-            run(stage_1b, i - 2)
-            run(functools.partial(stage_c, w, wdv), i - 1)
-            run(stage_1a, i - 1)
-            run(stage_2c, i - 4)
+            stage_a(w, wdv, i)
+            run(stage_2b, i - 3)
+            stage_b(w, wdv, i)
+            run(stage_1c, i - 2)
+            run(stage_2a, i - 2)
+            run(stage_1b, i - 1)
+            stage_c(w, wdv, i)
+            stage_1a(i)
+            run(stage_2c, i - 3)
             run(stage_3a, i - O3A)
             run(stage_3b, i - O3B)
             run(stage_4a, i - O4A)
@@ -349,7 +359,7 @@
 
     blocks = 2 * half // N
     tail = nch + O5
-    per_step = -(-blocks // (tail - nch - 1))
+    per_step = -(-blocks // (tail - nch))
 
     def weights(gr, xv, dv, gst, dst):
         load = pltpu.make_async_copy(grads, gr, g_sem)
@@ -413,15 +423,15 @@
 
         split = per_step // 2
 
-        @pl.loop(nch + 1, tail)
+        @pl.loop(nch, tail)
         def _(i):
-            j = (i - nch - 1) * per_step
-            run(stage_2b, i - 4)
-            run(stage_1c, i - 3)
-            run(stage_2a, i - 3)
-            run(stage_1b, i - 2)
+            j = (i - nch) * per_step
+            run(stage_2b, i - 3)
+            run(stage_1c, i - 2)
+            run(stage_2a, i - 2)
+            run(stage_1b, i - 1)
             units(j, j + split)
-            run(stage_2c, i - 4)
+            run(stage_2c, i - 3)
             run(stage_3a, i - O3A)
             run(stage_3b, i - O3B)
             units(j + split, j + per_step)
@@ -496,7 +506,7 @@
             pltpu.VMEM((2, 2, 2, sub, L), BF16),
             pltpu.VMEM((nch, 2, sub, L), BF16),
             dma((3,)),
-            dma((3,)),
+            dma((5,)),
             dma((2,)),
             dma((nch, 2)),
             dma((2, SIDE)),
@@ -518,7 +528,13 @@
     )(x, dy, gate, up, wg, wu, wd)
 
 
-def place_kernel(g, out):
+def place_kernel(g, wg_in, wu_in, wd_in, out, wg_out, wu_out, wd_out):
+    @pl.when(pl.program_id(1) == 0)
+    def _():
+        wg_out[...] = wg_in[...]
+        wu_out[...] = wu_in[...]
+        wd_out[...] = wd_in[...]
+
     for c in range(2):
         for a in range(SIDE):
             pieces = [g[0, 0, c, a, b] if c == 0 else g[0, 0, c, b, a] for b in range(SIDE)]
@@ -527,27 +543,42 @@
             out[0, pl.ds(c * L, L), pl.ds(a * n, n)] = stacked.T
 
 
-def place_call(whole):
+def place_call(whole, dwg, dwu, dwd):
     nch, _, _, _, _, sub, _ = whole.shape
     half = sub * SIDE * SIDE
+    d, f = dwg.shape
+    n = d // nch
+    tall = pl.BlockSpec((n, f), lambda k, c: (k, 0))
+    wide = pl.BlockSpec((f, n), lambda k, c: (0, k))
     return pl.pallas_call(
         place_kernel,
         grid=(nch, 2),
-        out_shape=jax.ShapeDtypeStruct((nch, R, 2 * half), BF16),
-        in_specs=[pl.BlockSpec((1, 1, 2, SIDE, SIDE, sub, L), lambda k, c: (k, c, 0, 0, 0, 0, 0))],
-        out_specs=pl.BlockSpec((1, R, half), lambda k, c: (k, 0, c)),
+        out_shape=[
+            jax.ShapeDtypeStruct((nch, R, d), BF16),
+            jax.ShapeDtypeStruct((d, f), BF16),
+            jax.ShapeDtypeStruct((d, f), BF16),
+            jax.ShapeDtypeStruct((f, d), BF16),
+        ],
+        in_specs=[
+            pl.BlockSpec((1, 1, 2, SIDE, SIDE, sub, L), lambda k, c: (k, c, 0, 0, 0, 0, 0)),
+            tall,
+            tall,
+            wide,
+        ],
+        out_specs=[pl.BlockSpec((1, R, half), lambda k, c: (k, 0, c)), tall, tall, wide],
         compiler_params=pltpu.CompilerParams(vmem_limit_bytes=60 * 2**20),
         cost_estimate=pl.CostEstimate(
-            flops=nch * R * half * 64, bytes_accessed=8 * nch * R * half, transcendentals=0
+            flops=nch * R * half * 64, bytes_accessed=8 * nch * R * half + 12 * d * f, transcendentals=0
         ),
         name="place",
-    )(whole)
+    )(whole, dwg, dwu, dwd)
 
 
 def solution(mesh):
     def step(x, dy, gate, up, w_gate, w_up, w_down):
-        _, whole, dw_gate, dw_up, dw_down = block_call(x, dy, gate, up, w_gate, w_up, w_down)
-        return place_call(whole).reshape(x.shape), dw_gate, dw_up, dw_down
+        _, whole, *grads = block_call(x, dy, gate, up, w_gate, w_up, w_down)
+        dx, *grads = place_call(whole, *grads)
+        return dx.reshape(x.shape), *grads
 
     tokens, columns, rows = P("dp", None), P(None, "tp"), P("tp", None)
     return jax.shard_map(

time: 273 us -> 256 us (0.938)
  local copies, waits for them, and re-layouts: 23.9 us -> 0 us
  Pallas kernels: 248 us -> 255 us
    unnamed x3 -> x0, local copies, waits for them, and re-layouts: 23.9 us -> none
    pallas_call x1, Pallas kernels: 27.4 us -> 47 us  [place_call(): pl.pallas_call(place_kernel, grid=(nch, 2), out_shape=[jax.ShapeDtypeStru...]
    pallas_call x1, Pallas kernels: 221 us -> 208 us  [block_call(): pl.pallas_call(functools.partial(block_kernel, nch), out_shape=[jax.Shape...]
where the time goes in v3:
time: 256 us
  Pallas kernels  255 us (100%)
    pallas_call x1, Pallas kernels, block_call(): pl.pallas_call(functools.partial(block_kernel, nch), out_shape=[jax.Shape...  208 us
    pallas_call x1, Pallas kernels, place_call(): pl.pallas_call(place_kernel, grid=(nch, 2), out_shape=[jax.ShapeDtypeStru...  47 us

profile of v3, /device:TPU:97, one launch (start us, length us, event | category | flops | bytes accessed | tf_op | source)
XLA Modules:
  0.0 256.0 jit_solution(13486879341797032520)
XLA Ops:
  0.6 208.3 %mlp_backward.1 = (bf16[1920,2048]{1,0:T(8,128)(2,1)}, bf16[8,2,2,4,4,224,128]{6,5,4,3,2,1,0:T(8,128)(2,1)}, bf16[7168,640]{1,0:T(8,128)(2,1)}, bf16[7168,640]{1,0:T(8,128)(2,1)}, bf16[640,7168]{1,0:T(8,128)(2,1)}) custom-call(bf16[2048,7168]{1,0:T(8,128)(2,1)} %x_in.1, bf16[2048,7168]{1,0:T(8,128)(2,1)} %dy.1, bf16[2048,640]{1,0:T(8,128)(2,1)} %gate.1, ...), custom_call_target="tpu_custom_call" | custom-call | flops 112742891520 | bytes 172490752 | tf_op jit(solution)/shard_map/mlp_backward/pallas_call | solution.py:478
  209.0 47.0 %place.1 = (bf16[8,256,7168]{2,1,0:T(8,128)(2,1)}, bf16[7168,640]{1,0:T(8,128)(2,1)}, bf16[7168,640]{1,0:T(8,128)(2,1)}, bf16[640,7168]{1,0:T(8,128)(2,1)}) custom-call(bf16[8,2,2,4,4,224,128]{6,5,4,3,2,1,0:T(8,128)(2,1)} %get-tuple-element.12.g, bf16[7168,640]{1,0:T(8,128)(2,1)} %get-tuple-element.13.wg_in, bf16[7168,640]{1,0:T(8,128)(2,1)} %get-tuple-element.14.wu_in, ...), custom_call_target="tpu_custom_call" | custom-call | flops 469762048 | bytes 113770496 | tf_op jit(solution)/shard_map/place/pallas_call | solution.py:553

commit v4 on v3

--- a/solution.py
+++ b/solution.py
@@ -281,9 +281,9 @@
         at4 = whole.at[k, core, c, came_from(pos1[c], d), pl.ds(2 * d, 2)]
         return spread(k, c, d, at4, at4, ss4b, sr4b, ring1)
 
-    def h5(k, c):
-        at5 = whole.at[k, core, c]
-        return remote(at5, at5, ss5.at[k, c], sr5.at[k, c], partner)
+    def h5(k, c, off):
+        at5 = whole.at[k, core, c, ring_at(pos1[c], off)]
+        return remote(at5, at5, ss5.at[k, c, off], sr5.at[k, c, off], partner)
 
     def stage_3a(k):
         for c in range(2):
@@ -303,17 +303,19 @@
                 h3b(k, c, d).wait_recv()
             for d in range(2):
                 h4a(k, c, d).start()
+            h5(k, c, 0).start()
 
     def stage_4b(k):
         for c, d in CD:
             h4a(k, c, d).wait_recv()
             h4b(k, c, d).start()
+            h5(k, c, SIDE - 1 if d == 0 else 1).start()
 
     def stage_5(k):
         for c in range(2):
             for d in range(2):
                 h4b(k, c, d).wait_recv()
-            h5(k, c).start()
+            h5(k, c, 2).start()
 
     def run(stage, k):
         @pl.when((k >= 0) & (k < nch))
@@ -465,7 +467,8 @@
             for c, d in CD:
                 h(k, c, d).wait_send()
         for c in range(2):
-            h5(k, c).wait()
+            for off in range(SIDE):
+                h5(k, c, off).wait()
 
 
 def block_call(x, dy, gate, up, wg, wu, wd):
@@ -514,7 +517,7 @@
         ]
         + [dma((2, 2, 2))] * 8
         + [dma((nch, 2, 2))] * 8
-        + [dma((nch, 2))] * 2
+        + [dma((nch, 2, SIDE))] * 2
         + [dma, dma((2, 2)), dma((2, 3))]
         + [pltpu.SemaphoreType.REGULAR]
         + [pltpu.SemaphoreType.REGULAR((2, 2))] * 4,
@@ -529,30 +532,28 @@
 
 
 def place_kernel(g, wg_in, wu_in, wd_in, out, wg_out, wu_out, wd_out):
-    @pl.when(pl.program_id(1) == 0)
-    def _():
-        wg_out[...] = wg_in[...]
-        wu_out[...] = wu_in[...]
-        wd_out[...] = wd_in[...]
-
-    for c in range(2):
-        for a in range(SIDE):
-            pieces = [g[0, 0, c, a, b] if c == 0 else g[0, 0, c, b, a] for b in range(SIDE)]
-            stacked = jnp.concatenate(pieces, axis=0)
-            n = stacked.shape[0]
-            out[0, pl.ds(c * L, L), pl.ds(a * n, n)] = stacked.T
+    wg_out[...] = wg_in[...]
+    wu_out[...] = wu_in[...]
+    wd_out[...] = wd_in[...]
+
+    for core in range(2):
+        for c in range(2):
+            for a in range(SIDE):
+                pieces = [g[0, core, c, a, b] if c == 0 else g[0, core, c, b, a] for b in range(SIDE)]
+                stacked = jnp.concatenate(pieces, axis=0)
+                n = stacked.shape[0]
+                out[0, pl.ds(c * L, L), pl.ds((core * SIDE + a) * n, n)] = stacked.T
 
 
 def place_call(whole, dwg, dwu, dwd):
     nch, _, _, _, _, sub, _ = whole.shape
-    half = sub * SIDE * SIDE
     d, f = dwg.shape
     n = d // nch
-    tall = pl.BlockSpec((n, f), lambda k, c: (k, 0))
-    wide = pl.BlockSpec((f, n), lambda k, c: (0, k))
+    tall = pl.BlockSpec((n, f), lambda k: (k, 0))
+    wide = pl.BlockSpec((f, n), lambda k: (0, k))
     return pl.pallas_call(
         place_kernel,
-        grid=(nch, 2),
+        grid=(nch,),
         out_shape=[
             jax.ShapeDtypeStruct((nch, R, d), BF16),
             jax.ShapeDtypeStruct((d, f), BF16),
@@ -560,15 +561,15 @@
             jax.ShapeDtypeStruct((f, d), BF16),
         ],
         in_specs=[
-            pl.BlockSpec((1, 1, 2, SIDE, SIDE, sub, L), lambda k, c: (k, c, 0, 0, 0, 0, 0)),
+            pl.BlockSpec((1, 2, 2, SIDE, SIDE, sub, L), lambda k: (k, 0, 0, 0, 0, 0, 0)),
             tall,
             tall,
             wide,
         ],
-        out_specs=[pl.BlockSpec((1, R, half), lambda k, c: (k, 0, c)), tall, tall, wide],
+        out_specs=[pl.BlockSpec((1, R, d), lambda k: (k, 0, 0)), tall, tall, wide],
         compiler_params=pltpu.CompilerParams(vmem_limit_bytes=60 * 2**20),
         cost_estimate=pl.CostEstimate(
-            flops=nch * R * half * 64, bytes_accessed=8 * nch * R * half + 12 * d * f, transcendentals=0
+            flops=nch * R * d * 32, bytes_accessed=4 * nch * R * d + 12 * d * f, transcendentals=0
         ),
         name="place",
     )(whole, dwg, dwu, dwd)

time: 256 us -> 244 us (0.953)
  Pallas kernels: 255 us -> 244 us
    pallas_call x1, Pallas kernels: 47 us -> 36.3 us  [place_call(): pl.pallas_call(place_kernel, grid=(nch,), out_shape=[jax.ShapeDtypeStruct...]
where the time goes in v4:
time: 244 us
  Pallas kernels  244 us (100%)
    pallas_call x1, Pallas kernels, block_call(): pl.pallas_call(functools.partial(block_kernel, nch), out_shape=[jax.Shape...  207 us
    pallas_call x1, Pallas kernels, place_call(): pl.pallas_call(place_kernel, grid=(nch,), out_shape=[jax.ShapeDtypeStruct...  36.3 us

profile of v4, /device:TPU:97, one launch (start us, length us, event | category | flops | bytes accessed | tf_op | source)
XLA Modules:
  0.0 244.2 jit_solution(2546727213353556626)
XLA Ops:
  0.6 207.2 %mlp_backward.1 = (bf16[1920,2048]{1,0:T(8,128)(2,1)}, bf16[8,2,2,4,4,224,128]{6,5,4,3,2,1,0:T(8,128)(2,1)}, bf16[7168,640]{1,0:T(8,128)(2,1)}, bf16[7168,640]{1,0:T(8,128)(2,1)}, bf16[640,7168]{1,0:T(8,128)(2,1)}) custom-call(bf16[2048,7168]{1,0:T(8,128)(2,1)} %x_in.1, bf16[2048,7168]{1,0:T(8,128)(2,1)} %dy.1, bf16[2048,640]{1,0:T(8,128)(2,1)} %gate.1, ...), custom_call_target="tpu_custom_call" | custom-call | flops 112742891520 | bytes 172490752 | tf_op jit(solution)/shard_map/mlp_backward/pallas_call | solution.py:481
  207.9 36.3 %place.1 = (bf16[8,256,7168]{2,1,0:T(8,128)(2,1)}, bf16[7168,640]{1,0:T(8,128)(2,1)}, bf16[7168,640]{1,0:T(8,128)(2,1)}, bf16[640,7168]{1,0:T(8,128)(2,1)}) custom-call(bf16[8,2,2,4,4,224,128]{6,5,4,3,2,1,0:T(8,128)(2,1)} %get-tuple-element.12.g, bf16[7168,640]{1,0:T(8,128)(2,1)} %get-tuple-element.13.wg_in, bf16[7168,640]{1,0:T(8,128)(2,1)} %get-tuple-element.14.wu_in, ...), custom_call_target="tpu_custom_call" | custom-call | flops 469762048 | bytes 113770496 | tf_op jit(solution)/shard_map/place/pallas_call | solution.py:554
